TPU v7x, 32 devices: a whole 2x2x4 slice. The times are simulated.
32 devices in a mesh: rve: 4 (over y, x), slab: 8 (over z, core).
Axes of the slice: x: 2, y: 2, z: 4, core: 2. Of those that a mesh axis runs over, the one named last changes fastest.
Arguments:
- displacement: float32 [32, 3, 128, 256], P('slab', None, 'rve'), parts along dimension 2, may hold values from -6 to 6
- load: float32 [32, 3, 128, 256], P('slab', None, 'rve'), parts along dimension 2, may hold values from -24 to 24
- phase: int32 [32, 128, 256], P('slab', 'rve'), parts along dimension 1, may hold values from 0 to 2
- moduli: float32 [2, 3], replicated, may hold values from 0.5 to 4
Outputs:
- solution: float32 [32, 3, 128, 256], P('slab', None, 'rve'), parts along dimension 2
- residual: float32 [32, 3, 128, 256], P('slab', None, 'rve'), parts along dimension 2
There are 4 independent parts, one for each index of `rve`. A program takes and returns all parts, laid end to end along the dimension named above; an argument that names none is the same for every part. Nothing has to cross between parts.
All inputs are finite; a program needn't handle non-finite values.
Results may differ from a plain program's by a relative error of at most 0.00002.
Values sent between devices are 32-bit elements; how exact they have to be, the bound alone decides.
A program may use at most 64 MiB of HBM per device.

v0:
```python
import jax
import jax.numpy as jnp
from jax import lax
from jax.sharding import PartitionSpec as P

SWEEPS = 6


def padded_2(array, sides, width):
    for axis, dim in sides:
        peers, length = (lax.axis_size(axis), array.shape[dim])
        up = [(i, (i + 1) % peers) for i in range(peers)]
        down = [(j, i) for i, j in up]
        last = lax.slice_in_dim(array, length - width, length, axis=dim)
        first = lax.slice_in_dim(array, 0, width, axis=dim)
        before = lax.ppermute(last, axis, up)
        after = lax.ppermute(first, axis, down)
        array = jnp.concatenate([before, array, after], axis=dim)
    return array


def plus_next(value, axis):
    return value + jnp.roll(value, -1, axis)


def minus_next(value, axis):
    return jnp.roll(value, -1, axis) - value


def plus_prev(value, axis):
    return value + jnp.roll(value, 1, axis)


def prev_minus(value, axis):
    return jnp.roll(value, 1, axis) - value


def materials(phase, moduli):
    lame = jnp.zeros(phase.shape, jnp.float32)
    shear = jnp.zeros(phase.shape, jnp.float32)
    for index in range(moduli.shape[1]):
        select = (phase == index).astype(jnp.float32)
        lame = lame + select * moduli[0, index]
        shear = shear + select * moduli[1, index]
    return (lame, shear)


def element_terms(lower, upper, lame, shear):
    total = lower + upper
    jump = upper - lower
    grad_x = 0.25 * minus_next(plus_next(total, -1), -2)
    grad_y = 0.25 * plus_next(minus_next(total, -1), -2)
    grad_z = 0.25 * plus_next(plus_next(jump, -1), -2)
    trace = grad_x[:, 0] + grad_y[:, 1] + grad_z[:, 2]
    normal_x = lame * trace + 2.0 * shear * grad_x[:, 0]
    normal_y = lame * trace + 2.0 * shear * grad_y[:, 1]
    normal_z = lame * trace + 2.0 * shear * grad_z[:, 2]
    shear_xy = shear * (grad_y[:, 0] + grad_x[:, 1])
    shear_xz = shear * (grad_z[:, 0] + grad_x[:, 2])
    shear_yz = shear * (grad_z[:, 1] + grad_y[:, 2])
    col_x = jnp.stack([normal_x, shear_xy, shear_xz], 1)
    col_y = jnp.stack([shear_xy, normal_y, shear_yz], 1)
    col_z = jnp.stack([shear_xz, shear_yz, normal_z], 1)
    inplane = 0.25 * (plus_prev(prev_minus(col_x, -2), -1) + plus_prev(prev_minus(col_y, -1), -2))
    vertical = 0.25 * plus_prev(plus_prev(col_z, -1), -2)
    return (inplane, vertical)


def apply_padded(field, lame_part, shear_part):
    inplane, vertical = element_terms(field[:-1], field[1:], lame_part, shear_part)
    return inplane[1:] + inplane[:-1] + vertical[:-1] - vertical[1:]


def field_padded(field):
    return padded_2(field, (("slab", 0),), 2)


def diagonal_of(lame_ext, shear_ext):
    stiff = lame_ext + 4.0 * shear_ext
    planar = plus_prev(plus_prev(stiff, -1), -2)
    return ((planar[1:] + planar[:-1]) / 16.0)[:, None]


def on_device(displacement, load, phase, moduli):
    lame, shear = materials(phase, moduli)
    stacked = jnp.concatenate([load, lame[:, None], shear[:, None]], 1)
    padded = padded_2(stacked, (("slab", 0),), 2)
    load_ext = padded[1:-1, 0:3]
    lame_ext = padded[:-1, 3]
    shear_ext = padded[:-1, 4]
    diagonal = diagonal_of(lame_ext, shear_ext)
    field = displacement
    for pair in range(SWEEPS // 2):
        wide = field_padded(field)
        wide = wide[1:-1] + 0.5 * (load_ext - apply_padded(wide, lame_ext, shear_ext)) / diagonal
        field = (
            wide[1:-1]
            + 0.5
            * (load_ext[1:-1] - apply_padded(wide, lame_ext[1:-1], shear_ext[1:-1]))
            / diagonal[1:-1]
        )
    wide = field_padded(field)[1:-1]
    remain = load_ext[1:-1] - apply_padded(wide, lame_ext[1:-1], shear_ext[1:-1])
    return (field, remain)


def solution(mesh):
    in_specs = (
        P("slab", None, "rve", None),
        P("slab", None, "rve", None),
        P("slab", "rve", None),
        P(),
    )
    out_specs = (P("slab", None, "rve", None), P("slab", None, "rve", None))
    return jax.shard_map(
        on_device, mesh=mesh, in_specs=in_specs, out_specs=out_specs, check_vma=False
    )
```

profile of v0, /device:TPU:0, one launch (start us, length us, event | category | flops | bytes accessed | tf_op | source)
XLA Modules:
  0.0 73.5 jit_solution(753766495912361569)
XLA Ops:
  0.6 1.1 %fusion.109 = (f32[2,3,32,256]{3,2,1,0:T(8,128)S(1)}, f32[2,3,32,256]{3,2,1,0:T(8,128)S(1)}) fusion(f32[4,3,32,256]{3,2,1,0:T(8,128)} %param.4), kind=kLoop, calls=%fused_computation.314 | loop fusion | bytes 786432 | tf_op jit(solution)/shard_map/slice | solution.py:15
  1.7 0.5 collective-permute-start
  2.3 1.6 %fusion.110 = (f32[1,1]{1,0:T(1,128)}, f32[1,1]{1,0:T(1,128)}, f32[1,1]{1,0:T(1,128)}, f32[1,1]{1,0:T(1,128)}, f32[1,1]{1,0:T(1,128)}, /*index=5*/f32[1,1]{1,0:T(1,128)}) fusion(f32[2,3]{1,0:T(2,128)} %param.7), kind=kLoop, calls=%fused_computation.315 | loop fusion | bytes 48 | tf_op jit(solution)/shard_map/slice | solution.py:44
  3.9 2.9 %add_bitcast_fusion.2 = (f32[4,1,32,256]{3,2,1,0:T(8,128)S(1)}, pred[4,32,256]{2,1,0:T(8,128)(4,1)S(1)}, pred[4,32,256]{2,1,0:T(8,128)(4,1)S(1)}, pred[4,32,256]{2,1,0:T(8,128)(4,1)S(1)}) fusion(f32[]{:T(128)} %bitcast.2, f32[]{:T(128)} %bitcast.1, f32[]{:T(128)} %bitcast, s32[4,32,256]{2,1,0:T(8,128)} %param.6), kind=kLoop, calls=%fused_computation.302 | loop fusion | flops 262144 | bytes 360460 | tf_op jit(solution)/shard_map/broadcast_in_dim | solution.py:86
  6.7 2.0 %add_bitcast_fusion.1 = f32[4,1,32,256]{3,2,1,0:T(8,128)S(1)} fusion(pred[4,32,256]{2,1,0:T(8,128)(4,1)S(1)} %get-tuple-element.24, pred[4,32,256]{2,1,0:T(8,128)(4,1)S(1)} %get-tuple-element.23, pred[4,32,256]{2,1,0:T(8,128)(4,1)S(1)} %get-tuple-element.22, f32[]{:T(128)} %bitcast.7, f32[]{:T(128)} %bitcast.6, f32[]{:T(128)} %bitcast.5), kind=kLoop, calls=%fused_computation.301 | loop fusion | flops 163840 | bytes 229388 | tf_op jit(solution)/shard_map/broadcast_in_dim | solution.py:86
  8.8 2.7 %collective-permute-start.2 = (f32[2,5,32,256]{3,2,1,0:T(8,128)S(1)}, f32[2,5,32,256]{3,2,1,0:T(8,128)S(1)}, u32[]{:S(2)}, u32[]{:S(2)}) collective-permute-start(f32[2,5,32,256]{3,2,1,0:T(8,128)S(1)} %get-tuple-element.70), channel_id=1, source_target_pairs={{0,1},{1,2},{2,3},{3,4},{4,5},{5,6},{6,7},{7,0},{8,9},{9,10},{10,1... | collective-permute-start | bytes 983048 | tf_op jit(solution)/shard_map/ppermute | solution.py:16
  11.6 1.4 %collective-permute-start.3 = (f32[2,5,32,256]{3,2,1,0:T(8,128)S(1)}, f32[2,5,32,256]{3,2,1,0:T(8,128)S(1)}, u32[]{:S(2)}, u32[]{:S(2)}) collective-permute-start(f32[2,5,32,256]{3,2,1,0:T(8,128)S(1)} %get-tuple-element.71), channel_id=1, source_target_pairs={{1,0},{2,1},{3,2},{4,3},{5,4},{6,5},{7,6},{0,7},{9,8},{10,9},{11,1... | collective-permute-start | bytes 983048 | tf_op jit(solution)/shard_map/ppermute | solution.py:17
  13.0 0.7 collective-permute-start.1
  13.8 7.4 %collective-permute-done.1 = f32[2,3,32,256]{3,2,1,0:T(8,128)S(1)} collective-permute-done((f32[2,3,32,256]{3,2,1,0:T(8,128)S(1)}, f32[2,3,32,256]{3,2,1,0:T(8,128)S(1)}, u32[]{:S(2)}, u32[]{:S(2)}) %collective-permute-start.1) | collective-permute-done | bytes 196640 | tf_op jit(solution)/shard_map/ppermute | solution.py:17
  21.3 0.2 slice.1259
  21.6 0.2 slice.1267
  21.9 0.2 maximum_add_fusion.1
  22.2 0.2 fusion.59
  22.8 0.3 fusion
  23.5 0.3 multiply_add_fusion.7
  23.9 0.3 pad_maximum_fusion.5
  24.5 0.5 maximum_subtract_fusion.2
  25.4 0.4 fusion.4
  25.9 0.3 fusion.29
  26.3 0.2 slice.1303
  26.7 0.2 slice.1311
  27.8 0.2 pad_maximum_fusion.20
  28.2 0.4 maximum_subtract_fusion.11
  28.9 0.3 fusion.34
  29.4 2.0 %collective-permute-start.4 = (f32[2,3,32,256]{3,2,1,0:T(8,128)S(1)}, f32[2,3,32,256]{3,2,1,0:T(8,128)S(1)}, u32[]{:S(2)}, u32[]{:S(2)}) collective-permute-start(f32[2,3,32,256]{3,2,1,0:T(8,128)S(1)} %get-tuple-element.88), channel_id=1, source_target_pairs={{0,1},{1,2},{2,3},{3,4},{4,5},{5,6},{6,7},{7,0},{8,9},{9,10},{10,1... | collective-permute-start | bytes 589832 | tf_op jit(solution)/shard_map/ppermute | solution.py:16
  31.4 2.0 %collective-permute-start.5 = (f32[2,3,32,256]{3,2,1,0:T(8,128)S(1)}, f32[2,3,32,256]{3,2,1,0:T(8,128)S(1)}, u32[]{:S(2)}, u32[]{:S(2)}) collective-permute-start(f32[2,3,32,256]{3,2,1,0:T(8,128)S(1)} %get-tuple-element.89), channel_id=1, source_target_pairs={{1,0},{2,1},{3,2},{4,3},{5,4},{6,5},{7,6},{0,7},{9,8},{10,9},{11,1... | collective-permute-start | bytes 589832 | tf_op jit(solution)/shard_map/ppermute | solution.py:17
  33.4 4.4 %collective-permute-done.4 = f32[2,3,32,256]{3,2,1,0:T(8,128)S(1)} collective-permute-done((f32[2,3,32,256]{3,2,1,0:T(8,128)S(1)}, f32[2,3,32,256]{3,2,1,0:T(8,128)S(1)}, u32[]{:S(2)}, u32[]{:S(2)}) %collective-permute-start.4) | collective-permute-done | bytes 196640 | tf_op jit(solution)/shard_map/ppermute | solution.py:16
  38.1 0.2 slice.1344
  38.4 0.2 fusion.57
  38.7 0.2 slice.1352
  39.0 0.2 maximum_add_fusion.8
  39.8 0.3 multiply_add_fusion.4
  40.1 0.3 pad_maximum_fusion.9
  40.8 0.5 maximum_subtract_fusion.5
  41.7 0.4 fusion.10
  42.0 0.3 fusion.25
  42.4 0.2 slice.1382
  42.9 0.2 slice.1390
  43.9 0.2 pad_maximum_fusion.24
  44.3 0.4 maximum_subtract_fusion.14
  45.0 0.3 fusion.40
  45.5 0.6 collective-permute-start.6
  46.1 2.9 %collective-permute-start.7 = (f32[2,3,32,256]{3,2,1,0:T(8,128)S(1)}, f32[2,3,32,256]{3,2,1,0:T(8,128)S(1)}, u32[]{:S(2)}, u32[]{:S(2)}) collective-permute-start(f32[2,3,32,256]{3,2,1,0:T(8,128)S(1)} %get-tuple-element.87), channel_id=1, source_target_pairs={{1,0},{2,1},{3,2},{4,3},{5,4},{6,5},{7,6},{0,7},{9,8},{10,9},{11,1... | collective-permute-start | bytes 589832 | tf_op jit(solution)/shard_map/ppermute | solution.py:17
  49.1 5.1 %collective-permute-done.6 = f32[2,3,32,256]{3,2,1,0:T(8,128)S(1)} collective-permute-done((f32[2,3,32,256]{3,2,1,0:T(8,128)S(1)}, f32[2,3,32,256]{3,2,1,0:T(8,128)S(1)}, u32[]{:S(2)}, u32[]{:S(2)}) %collective-permute-start.6) | collective-permute-done | bytes 196640 | tf_op jit(solution)/shard_map/ppermute | solution.py:16
  54.4 0.2 slice.1422
  54.6 0.2 fusion.55
  54.9 0.2 slice.1430
  55.2 0.2 maximum_add_fusion.15
  56.0 0.3 multiply_add_fusion.1
  56.4 0.3 pad_maximum_fusion.13
  57.0 0.5 maximum_subtract_fusion.8
  57.9 0.4 fusion.16
  58.3 0.3 fusion.21
  58.6 0.2 slice.1460
  59.1 0.2 slice.1468
  60.6 0.4 maximum_subtract_fusion.17
  61.2 0.3 fusion.46
  61.8 3.5 %collective-permute-start.9 = (f32[2,3,32,256]{3,2,1,0:T(8,128)S(1)}, f32[2,3,32,256]{3,2,1,0:T(8,128)S(1)}, u32[]{:S(2)}, u32[]{:S(2)}) collective-permute-start(f32[2,3,32,256]{3,2,1,0:T(8,128)S(1)} %get-tuple-element.84), channel_id=1, source_target_pairs={{1,0},{2,1},{3,2},{4,3},{5,4},{6,5},{7,6},{0,7},{9,8},{10,9},{11,1... | collective-permute-start | bytes 589832 | tf_op jit(solution)/shard_map/ppermute | solution.py:17
  65.3 4.4 %collective-permute-done.8 = f32[2,3,32,256]{3,2,1,0:T(8,128)S(1)} collective-permute-done((f32[2,3,32,256]{3,2,1,0:T(8,128)S(1)}, f32[2,3,32,256]{3,2,1,0:T(8,128)S(1)}, u32[]{:S(2)}, u32[]{:S(2)}) %collective-permute-start.8) | collective-permute-done | bytes 196640 | tf_op jit(solution)/shard_map/ppermute | solution.py:16
  69.9 0.2 slice.1497
  70.3 0.2 slice.1505
  71.8 0.4 maximum_subtract_fusion.20
  72.4 0.3 fusion.52
  72.7 0.8 %fusion.60 = f32[4,3,32,256]{3,2,1,0:T(8,128)} fusion(f32[4,3,32,256]{3,2,1,0:T(8,128)S(1)} %copy-done, f32[5,3,32,256]{3,2,1,0:T(8,128)S(1)} %fusion.53, f32[5,3,32,256]{3,2,1,0:T(8,128)S(1)} %fusion.52), kind=kLoop, calls=%fused_computation.186 | loop fusion | flops 393216 | bytes 2359296 | tf_op jit(solution)/shard_map/sub | solution.py:103
  (186 shorter events, 12.5 us)
Async XLA Ops:
  0.6 8.1 %copy-start = (f32[4,3,32,256]{3,2,1,0:T(8,128)S(1)}, f32[4,3,32,256]{3,2,1,0:T(8,128)}, u32[]{:S(2)}) copy-start(f32[4,3,32,256]{3,2,1,0:T(8,128)} %param.5) | copy-start | bytes 1179652
  1.7 11.9 %collective-permute-start = (f32[2,3,32,256]{3,2,1,0:T(8,128)S(1)}, f32[2,3,32,256]{3,2,1,0:T(8,128)S(1)}, u32[]{:S(2)}, u32[]{:S(2)}) collective-permute-start(f32[2,3,32,256]{3,2,1,0:T(8,128)S(1)} %get-tuple-element.91), channel_id=1, source_target_pairs={{0,1},{1,2},{2,3},{3,4},{4,5},{5,6},{6,7},{7,0},{8,9},{9,10},{10,1... | collective-permute-start | bytes 589832 | tf_op jit(solution)/shard_map/ppermute | solution.py:16
  8.7 5.0 %copy-start.2 = (f32[4,3,32,256]{3,2,1,0:T(8,128)S(1)}, f32[4,3,32,256]{3,2,1,0:T(8,128)}, u32[]{:S(2)}) copy-start(f32[4,3,32,256]{3,2,1,0:T(8,128)} %param.4) | copy-start | bytes 1179652
  8.8 14.2 %collective-permute-start.2 = (f32[2,5,32,256]{3,2,1,0:T(8,128)S(1)}, f32[2,5,32,256]{3,2,1,0:T(8,128)S(1)}, u32[]{:S(2)}, u32[]{:S(2)}) collective-permute-start(f32[2,5,32,256]{3,2,1,0:T(8,128)S(1)} %get-tuple-element.70), channel_id=1, source_target_pairs={{0,1},{1,2},{2,3},{3,4},{4,5},{5,6},{6,7},{7,0},{8,9},{9,10},{10,1... | collective-permute-start | bytes 983048 | tf_op jit(solution)/shard_map/ppermute | solution.py:16
  11.6 11.5 %collective-permute-start.3 = (f32[2,5,32,256]{3,2,1,0:T(8,128)S(1)}, f32[2,5,32,256]{3,2,1,0:T(8,128)S(1)}, u32[]{:S(2)}, u32[]{:S(2)}) collective-permute-start(f32[2,5,32,256]{3,2,1,0:T(8,128)S(1)} %get-tuple-element.71), channel_id=1, source_target_pairs={{1,0},{2,1},{3,2},{4,3},{5,4},{6,5},{7,6},{0,7},{9,8},{10,9},{11,1... | collective-permute-start | bytes 983048 | tf_op jit(solution)/shard_map/ppermute | solution.py:17
  13.0 8.2 %collective-permute-start.1 = (f32[2,3,32,256]{3,2,1,0:T(8,128)S(1)}, f32[2,3,32,256]{3,2,1,0:T(8,128)S(1)}, u32[]{:S(2)}, u32[]{:S(2)}) collective-permute-start(f32[2,3,32,256]{3,2,1,0:T(8,128)S(1)} %get-tuple-element.90), channel_id=1, source_target_pairs={{1,0},{2,1},{3,2},{4,3},{5,4},{6,5},{7,6},{0,7},{9,8},{10,9},{11,1... | collective-permute-start | bytes 589832 | tf_op jit(solution)/shard_map/ppermute | solution.py:17
  29.4 8.5 %collective-permute-start.4 = (f32[2,3,32,256]{3,2,1,0:T(8,128)S(1)}, f32[2,3,32,256]{3,2,1,0:T(8,128)S(1)}, u32[]{:S(2)}, u32[]{:S(2)}) collective-permute-start(f32[2,3,32,256]{3,2,1,0:T(8,128)S(1)} %get-tuple-element.88), channel_id=1, source_target_pairs={{0,1},{1,2},{2,3},{3,4},{4,5},{5,6},{6,7},{7,0},{8,9},{9,10},{10,1... | collective-permute-start | bytes 589832 | tf_op jit(solution)/shard_map/ppermute | solution.py:16
  31.4 6.5 %collective-permute-start.5 = (f32[2,3,32,256]{3,2,1,0:T(8,128)S(1)}, f32[2,3,32,256]{3,2,1,0:T(8,128)S(1)}, u32[]{:S(2)}, u32[]{:S(2)}) collective-permute-start(f32[2,3,32,256]{3,2,1,0:T(8,128)S(1)} %get-tuple-element.89), channel_id=1, source_target_pairs={{1,0},{2,1},{3,2},{4,3},{5,4},{6,5},{7,6},{0,7},{9,8},{10,9},{11,1... | collective-permute-start | bytes 589832 | tf_op jit(solution)/shard_map/ppermute | solution.py:17
  45.5 8.7 %collective-permute-start.6 = (f32[2,3,32,256]{3,2,1,0:T(8,128)S(1)}, f32[2,3,32,256]{3,2,1,0:T(8,128)S(1)}, u32[]{:S(2)}, u32[]{:S(2)}) collective-permute-start(f32[2,3,32,256]{3,2,1,0:T(8,128)S(1)} %get-tuple-element.86), channel_id=1, source_target_pairs={{0,1},{1,2},{2,3},{3,4},{4,5},{5,6},{6,7},{7,0},{8,9},{9,10},{10,1... | collective-permute-start | bytes 589832 | tf_op jit(solution)/shard_map/ppermute | solution.py:16
  46.1 8.0 %collective-permute-start.7 = (f32[2,3,32,256]{3,2,1,0:T(8,128)S(1)}, f32[2,3,32,256]{3,2,1,0:T(8,128)S(1)}, u32[]{:S(2)}, u32[]{:S(2)}) collective-permute-start(f32[2,3,32,256]{3,2,1,0:T(8,128)S(1)} %get-tuple-element.87), channel_id=1, source_target_pairs={{1,0},{2,1},{3,2},{4,3},{5,4},{6,5},{7,6},{0,7},{9,8},{10,9},{11,1... | collective-permute-start | bytes 589832 | tf_op jit(solution)/shard_map/ppermute | solution.py:17
  61.7 8.4 %copy-start.1 = (f32[4,3,32,256]{3,2,1,0:T(8,128)}, f32[4,3,32,256]{3,2,1,0:T(8,128)S(1)}, u32[]{:S(2)}) copy-start(f32[4,3,32,256]{3,2,1,0:T(8,128)S(1)} %fusion.64) | copy-start | bytes 1179652
  61.7 8.0 %collective-permute-start.8 = (f32[2,3,32,256]{3,2,1,0:T(8,128)S(1)}, f32[2,3,32,256]{3,2,1,0:T(8,128)S(1)}, u32[]{:S(2)}, u32[]{:S(2)}) collective-permute-start(f32[2,3,32,256]{3,2,1,0:T(8,128)S(1)} %get-tuple-element.85), channel_id=1, source_target_pairs={{0,1},{1,2},{2,3},{3,4},{4,5},{5,6},{6,7},{7,0},{8,9},{9,10},{10,1... | collective-permute-start | bytes 589832 | tf_op jit(solution)/shard_map/ppermute | solution.py:16
  61.8 8.0 %collective-permute-start.9 = (f32[2,3,32,256]{3,2,1,0:T(8,128)S(1)}, f32[2,3,32,256]{3,2,1,0:T(8,128)S(1)}, u32[]{:S(2)}, u32[]{:S(2)}) collective-permute-start(f32[2,3,32,256]{3,2,1,0:T(8,128)S(1)} %get-tuple-element.84), channel_id=1, source_target_pairs={{1,0},{2,1},{3,2},{4,3},{5,4},{6,5},{7,6},{0,7},{9,8},{10,9},{11,1... | collective-permute-start | bytes 589832 | tf_op jit(solution)/shard_map/ppermute | solution.py:17
where the time goes:
time: 73.8 us; the launch traced here: 73.5 us
  other arithmetic  22.4 us (30%)
  waiting for transfers between devices  21.4 us (29%)
  starting transfers between devices  16.6 us (22%)
  local copies, waits for them, and re-layouts  11 us (15%)
  between operations  2.2 us (3%)
    ppermute x5, waiting for transfers between devices, padded_2(): before = lax.ppermute(last, axis, up)  13.9 us
    ppermute x5, starting transfers between devices, padded_2(): after = lax.ppermute(first, axis, down)  10.6 us
    ppermute x5, waiting for transfers between devices, padded_2(): after = lax.ppermute(first, axis, down)  7.42 us
    ppermute x5, starting transfers between devices, padded_2(): before = lax.ppermute(last, axis, up)  6.01 us
    broadcast_in_dim x2, other arithmetic, on_device(): stacked = jnp.concatenate([load, lame[:, None], shear[:, None]], 1)  4.83 us
    slice x56, local copies, waits for them, and re-layouts, plus_next(): return value + jnp.roll(value, -1, axis)  4.21 us
    sub x7, other arithmetic, prev_minus(): return jnp.roll(value, 1, axis) - value  2.96 us
    add x14, other arithmetic, plus_next(): return value + jnp.roll(value, -1, axis)  2.38 us
  transfers between devices with their start and end apart: 10, of which 4 were waited for; matrix products, arithmetic and copies ran while one was open for 11% of the time, Pallas kernels for 0%

commit v1 on v0

v1 whole, which is shorter than its diff:
```python
import functools

import jax
import jax.numpy as jnp
from jax import lax
from jax.experimental import pallas as pl
from jax.experimental.pallas import tpu as pltpu
from jax.sharding import PartitionSpec as P

SWEEPS = 6
MESH = pl.DeviceIdType.MESH
ROWS = 8

STRESS = ((0, 3, 4), (3, 1, 5), (4, 5, 2))


def shift_next(value, axis):
    return pltpu.roll(value, value.shape[axis] - 1, axis)


def shift_prev(value, axis):
    return pltpu.roll(value, 1, axis)


def kernel(
    peers, disp, load, phase, moduli, out, rest,
    u, ld, ph, lam, mu, mu2, inv, fwd, st, res,
    in_sem, edge_send, edge_recv, send_sem, recv_sem, out_sem,
):
    local, _, nx, ny = disp.shape
    phases = moduli.shape[1]
    me = lax.axis_index("slab")
    above = lax.rem(me + 1, peers)
    below = lax.rem(me + peers - 1, peers)

    first = pltpu.make_async_copy(disp, u.at[0, pl.ds(2, local)], in_sem.at[0])
    second = pltpu.make_async_copy(phase, ph.at[pl.ds(2, local)], in_sem.at[1])
    third = pltpu.make_async_copy(load, ld.at[pl.ds(1, local)], in_sem.at[2])
    first.start()
    second.start()
    third.start()

    barrier = pltpu.get_barrier_semaphore()
    for peer in (below, above):
        pl.semaphore_signal(barrier, inc=1, device_id={"slab": peer}, device_id_type=MESH)
    pl.semaphore_wait(barrier, 2)

    edges = []

    def edge(src, dst, peer):
        at = len(edges)
        copy = pltpu.make_async_remote_copy(
            src_ref=src, dst_ref=dst, send_sem=edge_send.at[at], recv_sem=edge_recv.at[at],
            device_id={"slab": peer}, device_id_type=MESH,
        )
        copy.start()
        edges.append(copy)
        return copy

    first.wait()
    near_u = [edge(u.at[0, local + 1], u.at[0, 1], above), edge(u.at[0, 2], u.at[0, local + 2], below)]
    second.wait()
    near_ph = [edge(ph.at[local + 1], ph.at[1], above), edge(ph.at[2], ph.at[local + 2], below)]
    far_u = [edge(u.at[0, local], u.at[0, 0], above), edge(u.at[0, 3], u.at[0, local + 3], below)]
    far_ph = [edge(ph.at[local], ph.at[0], above)]
    third.wait()
    far_ld = [edge(ld.at[local], ld.at[0], above), edge(ld.at[1], ld.at[local + 1], below)]

    def sent(sweep, way):
        src, dst, peer = ((local, 0, above), (3, local + 3, below))[way]
        return pltpu.make_async_remote_copy(
            src_ref=u.at[sweep, src], dst_ref=u.at[sweep, dst],
            send_sem=send_sem.at[sweep, way], recv_sem=recv_sem.at[sweep, way],
            device_id={"slab": peer}, device_id_type=MESH,
        )

    def material(k):
        for r in range(0, nx, ROWS):
            at = pl.ds(r, ROWS)
            kind = ph[k + 2, at, :]
            lame = jnp.zeros(kind.shape, jnp.float32)
            shear = jnp.zeros(kind.shape, jnp.float32)
            for index in range(phases):
                lame = jnp.where(kind == index, moduli[0, index] * 0.0625, lame)
                shear = jnp.where(kind == index, moduli[1, index] * 0.0625, shear)
            lam[k + 2, at, :] = lame
            mu[k + 2, at, :] = shear
            mu2[k + 2, at, :] = shear + shear

    def diagonal(n):
        total = (lam[n + 1] + 2.0 * mu2[n + 1]) + (lam[n + 2] + 2.0 * mu2[n + 2])
        total = total + shift_prev(total, 1)
        total = total + shift_prev(total, 0)
        inv[n + 1] = 0.5 / total

    def forward(sweep, n):
        for c in range(3):
            value = u[sweep, n + 2, c]
            moved = shift_next(value, 1)
            total, jump = value + moved, moved - value
            moved = shift_next(total, 0)
            fwd[n + 2, c] = moved - total
            fwd[n + 2, 6 + c] = moved + total
            fwd[n + 2, 3 + c] = jump + shift_next(jump, 0)

    def element(k):
        lo, hi = k + 2, k + 3
        for r in range(0, nx, ROWS):
            at = pl.ds(r, ROWS)
            gx = [fwd[lo, c, at, :] + fwd[hi, c, at, :] for c in range(3)]
            gy = [fwd[lo, 3 + c, at, :] + fwd[hi, 3 + c, at, :] for c in range(3)]
            gz = [fwd[hi, 6 + c, at, :] - fwd[lo, 6 + c, at, :] for c in range(3)]
            bulk = lam[lo, at, :] * (gx[0] + gy[1] + gz[2])
            two, one = mu2[lo, at, :], mu[lo, at, :]
            st[lo, 0, at, :] = bulk + two * gx[0]
            st[lo, 1, at, :] = bulk + two * gy[1]
            st[lo, 2, at, :] = bulk + two * gz[2]
            st[lo, 3, at, :] = one * (gy[0] + gx[1])
            st[lo, 4, at, :] = one * (gz[0] + gx[2])
            st[lo, 5, at, :] = one * (gz[1] + gy[2])

    def remain(n, c):
        lo, hi = n + 1, n + 2
        x, y, z = STRESS[c]
        px = st[lo, x] + st[hi, x]
        rz = st[lo, z] - st[hi, z]
        qy = st[lo, y] + st[hi, y]
        e = (rz - px) + shift_prev(rz + px, 0)
        b = qy + shift_prev(qy, 0)
        return ld[n + 1, c] - ((e - b) + shift_prev(e + b, 1))

    def advance(sweep, n):
        for c in range(3):
            u[sweep, n + 2, c] = u[sweep - 1, n + 2, c] + inv[n + 1] * remain(n, c)

    def finish(n):
        for c in range(3):
            res[n, c] = remain(n, c)

    def inner(sweep):
        for n in range(local):
            forward(sweep - 1, n)
        for k in range(local - 1):
            element(k)

    def halo(sweep):
        forward(sweep - 1, -2)
        element(-2)
        advance(sweep, -1)
        forward(sweep - 1, local + 1)
        element(local)
        advance(sweep, local)

    def rim(sweep):
        forward(sweep, -1)
        element(-1)
        forward(sweep, local)
        element(local - 1)

    for k in range(local):
        material(k)
    for n in range(1, local):
        diagonal(n)
    inner(1)
    for n in range(1, local - 1):
        advance(1, n)
    for way in range(2):
        sent(1, way).start()
    for copy in near_u + near_ph:
        copy.wait_recv()
    material(-1)
    material(local)
    diagonal(0)
    diagonal(local)
    rim(0)
    advance(1, 0)
    advance(1, local - 1)

    def step(sweep, _):
        inner(sweep)
        for n in range(1, local - 1):
            advance(sweep, n)

        @pl.when(sweep < SWEEPS)
        def _():
            for way in range(2):
                sent(sweep, way).start()

        @pl.when(sweep == 2)
        def _():
            for copy in far_u + far_ph + far_ld:
                copy.wait_recv()
            material(-2)
            diagonal(-1)

        @pl.when(sweep > 2)
        def _():
            for way in range(2):
                sent(sweep - 2, way).wait_recv()

        halo(sweep - 1)
        rim(sweep - 1)
        advance(sweep, 0)
        advance(sweep, local - 1)
        return 0

    lax.fori_loop(2, SWEEPS + 1, step, 0)
    field_out = pltpu.make_async_copy(u.at[SWEEPS, pl.ds(2, local)], out, out_sem.at[0])
    field_out.start()

    inner(SWEEPS + 1)
    for n in range(1, local - 1):
        finish(n)
    for way in range(2):
        sent(SWEEPS - 1, way).wait_recv()
    halo(SWEEPS)
    rim(SWEEPS)
    finish(0)
    finish(local - 1)
    rest_out = pltpu.make_async_copy(res, rest, out_sem.at[1])
    rest_out.start()
    for copy in edges:
        copy.wait_send()
    for sweep in range(1, SWEEPS):
        for way in range(2):
            sent(sweep, way).wait_send()
    field_out.wait()
    rest_out.wait()


def on_device(peers, displacement, load, phase, moduli):
    local, comps, nx, ny = displacement.shape
    plane = (nx, ny)
    hbm = pl.BlockSpec(memory_space=pl.ANY)
    f32 = jnp.float32
    return pl.pallas_call(
        functools.partial(kernel, peers),
        out_shape=[jax.ShapeDtypeStruct(displacement.shape, f32)] * 2,
        in_specs=[hbm, hbm, hbm, pl.BlockSpec(memory_space=pltpu.SMEM)],
        out_specs=[hbm, hbm],
        scratch_shapes=[
            pltpu.VMEM((SWEEPS + 1, local + 4, comps) + plane, f32),
            pltpu.VMEM((local + 2, comps) + plane, f32),
            pltpu.VMEM((local + 3,) + plane, jnp.int32),
            pltpu.VMEM((local + 3,) + plane, f32),
            pltpu.VMEM((local + 3,) + plane, f32),
            pltpu.VMEM((local + 3,) + plane, f32),
            pltpu.VMEM((local + 2,) + plane, f32),
            pltpu.VMEM((local + 4, 9) + plane, f32),
            pltpu.VMEM((local + 3, 6) + plane, f32),
            pltpu.VMEM((local, comps) + plane, f32),
            pltpu.SemaphoreType.DMA((3,)),
            pltpu.SemaphoreType.DMA((9,)),
            pltpu.SemaphoreType.DMA((9,)),
            pltpu.SemaphoreType.DMA((SWEEPS + 1, 2)),
            pltpu.SemaphoreType.DMA((SWEEPS + 1, 2)),
            pltpu.SemaphoreType.DMA((2,)),
        ],
        compiler_params=pltpu.CompilerParams(collective_id=0, has_side_effects=True),
    )(displacement, load, phase, moduli)


def solution(mesh):
    in_specs = (
        P("slab", None, "rve", None),
        P("slab", None, "rve", None),
        P("slab", "rve", None),
        P(),
    )
    out_specs = (P("slab", None, "rve", None), P("slab", None, "rve", None))
    return jax.shard_map(
        functools.partial(on_device, mesh.shape["slab"]),
        mesh=mesh, in_specs=in_specs, out_specs=out_specs, check_vma=False,
    )
```

time: 73.8 us -> 30.6 us (0.41)
  Pallas kernels: 0 us -> 27.2 us
  other arithmetic: 22.4 us -> 0 us
  waiting for transfers between devices: 21.4 us -> 0 us
  starting transfers between devices: 16.6 us -> 0 us
  local copies, waits for them, and re-layouts: 11 us -> 2.57 us
  between operations: 2.2 us -> 0.65 us
    pallas_call x0 -> x1, Pallas kernels: none -> 27.2 us  [on_device(): pl.pallas_call(functools.partial(kernel, peers), out_shape=[jax.ShapeDtyp...]
    ppermute x10 -> x0, waiting for transfers between devices: 21.4 us -> none  [the longest x5 13.9 us: padded_2(): before = lax.ppermute(last, axis, up)]
    ppermute x10 -> x0, starting transfers between devices: 16.6 us -> none  [the longest x5 10.6 us: padded_2(): after = lax.ppermute(first, axis, down)]
    slice x121 -> x0, local copies, waits for them, and re-layouts: 10.9 us -> none  [the longest x56 4.21 us: plus_next(): return value + jnp.roll(value, -1, axis)]
    add x37 -> x0, other arithmetic: 5.85 us -> none  [the longest x14 2.38 us: plus_next(): return value + jnp.roll(value, -1, axis)]
    mul x34 -> x0, other arithmetic: 5.28 us -> none  [the longest x7 2.23 us: element_terms(): 0.25 * (plus_prev(prev_minus(col_x, -2), -1) + plus_prev(prev_minus(col_y...]
    broadcast_in_dim x2 -> x0, other arithmetic: 4.83 us -> none  [on_device(): stacked = jnp.concatenate([load, lame[:, None], shear[:, None]], 1)]
    sub x15 -> x0, other arithmetic: 4.59 us -> none  [the longest x7 2.96 us: prev_minus(): return jnp.roll(value, 1, axis) - value]
  transfers between devices with their start and end apart: 10 -> 0, of which waited for: 4 -> 0; matrix products, arithmetic and copies ran while one was open for 11% -> 0% of each run, Pallas kernels for 0% -> 0%
where the time goes in v1:
time: 30.6 us; the launch traced here: 30.4 us
  Pallas kernels  27.2 us (89%)
  local copies, waits for them, and re-layouts  2.57 us (8%)
  between operations  0.65 us (2%)
    pallas_call x1, Pallas kernels, on_device(): pl.pallas_call(functools.partial(kernel, peers), out_shape=[jax.ShapeDtyp...  27.2 us
    unnamed x4, local copies, waits for them, and re-layouts  2.57 us

profile of v1, /device:TPU:0, one launch (start us, length us, event | category | flops | bytes accessed | tf_op | source)
XLA Modules:
  0.0 30.4 jit_solution(4054721928593108621)
XLA Ops:
  0.6 27.2 %shard_map.59 = (f32[4,3,32,256]{3,2,1,0:T(8,128)}, f32[4,3,32,256]{3,2,1,0:T(8,128)}) custom-call(f32[4,3,32,256]{3,2,1,0:T(8,128)} %disp.1, f32[4,3,32,256]{3,2,1,0:T(8,128)} %load.1, s32[4,32,256]{2,1,0:T(8,128)} %phase.1, f32[2,3]{1,0:T(2,128)} %moduli.1), custom_call_target="tpu_custom_call" | custom-call | tf_op jit(solution)/shard_map/pallas_call | solution.py:236
  27.8 0.0 copy-start
  27.9 1.8 %copy.8 = f32[4,3,32,256]{3,2,1,0:T(8,128)} copy(f32[4,3,32,256]{3,2,1,0:T(8,128)} %get-tuple-element.4) | data formatting | bytes 786432
  29.7 0.0 copy-done
  29.7 0.7 %copy.9 = f32[4,3,32,256]{3,2,1,0:T(8,128)} copy(f32[4,3,32,256]{3,2,1,0:T(8,128)S(1)} %copy-done) | data formatting | bytes 786432
Async XLA Ops:
  27.8 1.8 %copy-start = (f32[4,3,32,256]{3,2,1,0:T(8,128)S(1)}, f32[4,3,32,256]{3,2,1,0:T(8,128)}, u32[]{:S(2)}) copy-start(f32[4,3,32,256]{3,2,1,0:T(8,128)} %get-tuple-element.5) | copy-start | bytes 1179652

commit v2 on v1

--- a/solution.py
+++ b/solution.py
@@ -24,8 +24,8 @@
 
 def kernel(
     peers, disp, load, phase, moduli, out, rest,
-    u, ld, ph, lam, mu, mu2, inv, fwd, st, res,
-    in_sem, edge_send, edge_recv, send_sem, recv_sem, out_sem,
+    u, ld, ph, lam, mu, mu2, inv, fwd, st,
+    in_sem, edge_send, edge_recv, send_sem, recv_sem,
 ):
     local, _, nx, ny = disp.shape
     phases = moduli.shape[1]
@@ -135,7 +135,7 @@
 
     def finish(n):
         for c in range(3):
-            res[n, c] = remain(n, c)
+            rest[n, c] = remain(n, c)
 
     def inner(sweep):
         for n in range(local):
@@ -143,19 +143,16 @@
         for k in range(local - 1):
             element(k)
 
-    def halo(sweep):
-        forward(sweep - 1, -2)
-        element(-2)
-        advance(sweep, -1)
-        forward(sweep - 1, local + 1)
-        element(local)
-        advance(sweep, local)
-
-    def rim(sweep):
-        forward(sweep, -1)
-        element(-1)
-        forward(sweep, local)
-        element(local - 1)
+    def halo(sweep, side):
+        forward(sweep - 1, (-2, local + 1)[side])
+        element((-2, local)[side])
+        advance(sweep, (-1, local)[side])
+
+    def rim(sweep, side):
+        forward(sweep, (-1, local)[side])
+        element((-1, local - 1)[side])
+
+    rims = (0, local - 1)
 
     for k in range(local):
         material(k)
@@ -166,15 +163,13 @@
         advance(1, n)
     for way in range(2):
         sent(1, way).start()
-    for copy in near_u + near_ph:
-        copy.wait_recv()
-    material(-1)
-    material(local)
-    diagonal(0)
-    diagonal(local)
-    rim(0)
-    advance(1, 0)
-    advance(1, local - 1)
+    for side in range(2):
+        near_u[side].wait_recv()
+        near_ph[side].wait_recv()
+        material((-1, local)[side])
+        diagonal((0, local)[side])
+        rim(0, side)
+        advance(1, rims[side])
 
     def step(sweep, _):
         inner(sweep)
@@ -186,46 +181,52 @@
             for way in range(2):
                 sent(sweep, way).start()
 
-        @pl.when(sweep == 2)
-        def _():
-            for copy in far_u + far_ph + far_ld:
-                copy.wait_recv()
-            material(-2)
-            diagonal(-1)
-
-        @pl.when(sweep > 2)
-        def _():
-            for way in range(2):
-                sent(sweep - 2, way).wait_recv()
-
-        halo(sweep - 1)
-        rim(sweep - 1)
-        advance(sweep, 0)
-        advance(sweep, local - 1)
+        for side in range(2):
+
+            @pl.when(sweep == 2)
+            def _():
+                far_u[side].wait_recv()
+                far_ld[side].wait_recv()
+                if side == 0:
+                    far_ph[0].wait_recv()
+                    material(-2)
+                    diagonal(-1)
+
+            @pl.when(sweep > 2)
+            def _():
+                sent(sweep - 2, side).wait_recv()
+
+            halo(sweep - 1, side)
+            rim(sweep - 1, side)
+            advance(sweep, rims[side])
         return 0
 
     lax.fori_loop(2, SWEEPS + 1, step, 0)
-    field_out = pltpu.make_async_copy(u.at[SWEEPS, pl.ds(2, local)], out, out_sem.at[0])
-    field_out.start()
-
+    for n in range(1, local - 1):
+        out[n] = u[SWEEPS, n + 2]
+    out[0] = u[SWEEPS, 2]
+    out[local - 1] = u[SWEEPS, local + 1]
     inner(SWEEPS + 1)
     for n in range(1, local - 1):
         finish(n)
-    for way in range(2):
-        sent(SWEEPS - 1, way).wait_recv()
-    halo(SWEEPS)
-    rim(SWEEPS)
-    finish(0)
-    finish(local - 1)
-    rest_out = pltpu.make_async_copy(res, rest, out_sem.at[1])
-    rest_out.start()
+    for side in range(2):
+        sent(SWEEPS - 1, side).wait_recv()
+        halo(SWEEPS, side)
+        rim(SWEEPS, side)
+        finish(rims[side])
     for copy in edges:
         copy.wait_send()
     for sweep in range(1, SWEEPS):
         for way in range(2):
             sent(sweep, way).wait_send()
-    field_out.wait()
-    rest_out.wait()
+
+
+def write_out(field, remain, out, rest, sem):
+    copies = [pltpu.make_async_copy(field, out, sem.at[0]), pltpu.make_async_copy(remain, rest, sem.at[1])]
+    for copy in copies:
+        copy.start()
+    for copy in copies:
+        copy.wait()
 
 
 def on_device(peers, displacement, load, phase, moduli):
@@ -233,11 +234,12 @@
     plane = (nx, ny)
     hbm = pl.BlockSpec(memory_space=pl.ANY)
     f32 = jnp.float32
-    return pl.pallas_call(
+    vmem = pl.BlockSpec(memory_space=pltpu.VMEM)
+    held = pl.pallas_call(
         functools.partial(kernel, peers),
-        out_shape=[jax.ShapeDtypeStruct(displacement.shape, f32)] * 2,
+        out_shape=[pltpu.VMEM(displacement.shape, f32)] * 2,
         in_specs=[hbm, hbm, hbm, pl.BlockSpec(memory_space=pltpu.SMEM)],
-        out_specs=[hbm, hbm],
+        out_specs=[vmem, vmem],
         scratch_shapes=[
             pltpu.VMEM((SWEEPS + 1, local + 4, comps) + plane, f32),
             pltpu.VMEM((local + 2, comps) + plane, f32),
@@ -248,16 +250,21 @@
             pltpu.VMEM((local + 2,) + plane, f32),
             pltpu.VMEM((local + 4, 9) + plane, f32),
             pltpu.VMEM((local + 3, 6) + plane, f32),
-            pltpu.VMEM((local, comps) + plane, f32),
             pltpu.SemaphoreType.DMA((3,)),
             pltpu.SemaphoreType.DMA((9,)),
             pltpu.SemaphoreType.DMA((9,)),
             pltpu.SemaphoreType.DMA((SWEEPS + 1, 2)),
             pltpu.SemaphoreType.DMA((SWEEPS + 1, 2)),
-            pltpu.SemaphoreType.DMA((2,)),
         ],
         compiler_params=pltpu.CompilerParams(collective_id=0, has_side_effects=True),
     )(displacement, load, phase, moduli)
+    return pl.pallas_call(
+        write_out,
+        out_shape=[jax.ShapeDtypeStruct(displacement.shape, f32)] * 2,
+        in_specs=[hbm, hbm],
+        out_specs=[hbm, hbm],
+        scratch_shapes=[pltpu.SemaphoreType.DMA((2,))],
+    )(*[pltpu.with_memory_space_constraint(one, pltpu.VMEM) for one in held])
 
 
 def solution(mesh):

time: 30.6 us -> 28.5 us (0.931)
  local copies, waits for them, and re-layouts: 2.57 us -> 0 us
  Pallas kernels: 27.2 us -> 27.7 us
    unnamed x4 -> x0, local copies, waits for them, and re-layouts: 2.57 us -> none
    pallas_call x1 -> x2, Pallas kernels: 27.2 us -> 27.7 us  [the longest x1 26.8 us: on_device(): pl.pallas_call(functools.partial(kernel, peers), out_shape=[pltpu.VMEM(di...]
where the time goes in v2:
time: 28.5 us; the launch traced here: 28.3 us
  Pallas kernels  27.7 us (97%)
  between operations  0.64 us (2%)
    pallas_call x1, Pallas kernels, on_device(): pl.pallas_call(functools.partial(kernel, peers), out_shape=[pltpu.VMEM(di...  26.8 us
    pallas_call x1, Pallas kernels, on_device(): pl.pallas_call(write_out, out_shape=[jax.ShapeDtypeStruct(displacement.sh...  0.89 us

profile of v2, /device:TPU:0, one launch (start us, length us, event | category | flops | bytes accessed | tf_op | source)
XLA Modules:
  0.0 28.3 jit_solution(6080437095714723278)
XLA Ops:
  0.6 26.8 %shard_map.59 = (f32[4,3,32,256]{3,2,1,0:T(8,128)S(1)}, f32[4,3,32,256]{3,2,1,0:T(8,128)S(1)}) custom-call(f32[4,3,32,256]{3,2,1,0:T(8,128)} %disp.1, f32[4,3,32,256]{3,2,1,0:T(8,128)} %load.1, s32[4,32,256]{2,1,0:T(8,128)} %phase.1, f32[2,3]{1,0:T(2,128)} %moduli.1), custom_call_target="tpu_custom_call" | custom-call | tf_op jit(solution)/shard_map/pallas_call | solution.py:238
  27.4 0.9 %shard_map.60 = (f32[4,3,32,256]{3,2,1,0:T(8,128)}, f32[4,3,32,256]{3,2,1,0:T(8,128)}) custom-call(f32[4,3,32,256]{3,2,1,0:T(8,128)S(1)} %get-tuple-element.4.field, f32[4,3,32,256]{3,2,1,0:T(8,128)S(1)} %get-tuple-element.5.remain), custom_call_target="tpu_custom_call" | custom-call | tf_op jit(solution)/shard_map/pallas_call | solution.py:261

commit v3 on v2

--- a/solution.py
+++ b/solution.py
@@ -53,18 +53,34 @@
             src_ref=src, dst_ref=dst, send_sem=edge_send.at[at], recv_sem=edge_recv.at[at],
             device_id={"slab": peer}, device_id_type=MESH,
         )
-        copy.start()
         edges.append(copy)
         return copy
 
-    first.wait()
     near_u = [edge(u.at[0, local + 1], u.at[0, 1], above), edge(u.at[0, 2], u.at[0, local + 2], below)]
-    second.wait()
     near_ph = [edge(ph.at[local + 1], ph.at[1], above), edge(ph.at[2], ph.at[local + 2], below)]
     far_u = [edge(u.at[0, local], u.at[0, 0], above), edge(u.at[0, 3], u.at[0, local + 3], below)]
     far_ph = [edge(ph.at[local], ph.at[0], above)]
+    far_ld = [edge(ld.at[local], ld.at[0], above), edge(ld.at[1], ld.at[local + 1], below)]
+    closing = (me == peers - 1, me == 0)
+
+    def far(way):
+        far_u[way].start()
+        if way == 0:
+            far_ph[0].start()
+        far_ld[way].start()
+
+    first.wait()
+    for copy in near_u:
+        copy.start()
+    second.wait()
+    for copy in near_ph:
+        copy.start()
     third.wait()
-    far_ld = [edge(ld.at[local], ld.at[0], above), edge(ld.at[1], ld.at[local + 1], below)]
+    for way in range(2):
+
+        @pl.when(closing[way])
+        def _():
+            far(way)
 
     def sent(sweep, way):
         src, dst, peer = ((local, 0, above), (3, local + 3, below))[way]
@@ -137,11 +153,18 @@
         for c in range(3):
             rest[n, c] = remain(n, c)
 
-    def inner(sweep):
-        for n in range(local):
-            forward(sweep - 1, n)
-        for k in range(local - 1):
+    rims = (0, local - 1)
+    seconds = (1, local - 2)
+
+    def middle(sweep):
+        for n in range(1, local - 1):
+            forward(sweep, n)
+        for k in range(1, local - 2):
             element(k)
+
+    def join(sweep, side):
+        forward(sweep, rims[side])
+        element((0, local - 2)[side])
 
     def halo(sweep, side):
         forward(sweep - 1, (-2, local + 1)[side])
@@ -152,35 +175,47 @@
         forward(sweep, (-1, local)[side])
         element((-1, local - 1)[side])
 
-    rims = (0, local - 1)
-
     for k in range(local):
         material(k)
     for n in range(1, local):
         diagonal(n)
-    inner(1)
+    middle(0)
+    for side in range(2):
+        join(0, side)
     for n in range(1, local - 1):
         advance(1, n)
     for way in range(2):
-        sent(1, way).start()
+
+        @pl.when(closing[way])
+        def _():
+            sent(1, way).start()
+
+    middle(1)
+    for n in range(2, local - 2):
+        advance(2, n)
     for side in range(2):
         near_u[side].wait_recv()
         near_ph[side].wait_recv()
         material((-1, local)[side])
         diagonal((0, local)[side])
+        if side == 0:
+            for way in range(2):
+
+                @pl.when(jnp.logical_not(closing[way]))
+                def _():
+                    far(way)
+                    sent(1, way).start()
+
         rim(0, side)
         advance(1, rims[side])
+        join(1, side)
+        advance(2, seconds[side])
+        sent(2, 1 - side).start()
 
     def step(sweep, _):
-        inner(sweep)
-        for n in range(1, local - 1):
-            advance(sweep, n)
-
-        @pl.when(sweep < SWEEPS)
-        def _():
-            for way in range(2):
-                sent(sweep, way).start()
-
+        middle(sweep)
+        for n in range(2, local - 2):
+            advance(sweep + 1, n)
         for side in range(2):
 
             @pl.when(sweep == 2)
@@ -199,16 +234,31 @@
             halo(sweep - 1, side)
             rim(sweep - 1, side)
             advance(sweep, rims[side])
+            join(sweep, side)
+            advance(sweep + 1, seconds[side])
+
+            @pl.when(sweep + 1 < SWEEPS)
+            def _():
+                sent(sweep + 1, 1 - side).start()
+
         return 0
 
-    lax.fori_loop(2, SWEEPS + 1, step, 0)
+    lax.fori_loop(2, SWEEPS, step, 0)
+
+    middle(SWEEPS)
+    for n in range(2, local - 2):
+        finish(n)
     for n in range(1, local - 1):
         out[n] = u[SWEEPS, n + 2]
-    out[0] = u[SWEEPS, 2]
-    out[local - 1] = u[SWEEPS, local + 1]
-    inner(SWEEPS + 1)
-    for n in range(1, local - 1):
-        finish(n)
+    for side in range(2):
+        sent(SWEEPS - 2, side).wait_recv()
+        halo(SWEEPS - 1, side)
+        rim(SWEEPS - 1, side)
+        advance(SWEEPS, rims[side])
+        join(SWEEPS, side)
+        finish(seconds[side])
+    for n in rims:
+        out[n] = u[SWEEPS, n + 2]
     for side in range(2):
         sent(SWEEPS - 1, side).wait_recv()
         halo(SWEEPS, side)

time: 28.5 us -> 27.7 us (0.972)
  Pallas kernels: 27.7 us -> 26.9 us
    pallas_call x1, Pallas kernels: 26.8 us -> 26 us  [on_device(): pl.pallas_call(functools.partial(kernel, peers), out_shape=[pltpu.VMEM(di...]
where the time goes in v3:
time: 27.7 us; the launch traced here: 27.5 us
  Pallas kernels  26.9 us (97%)
  between operations  0.64 us (2%)
    pallas_call x1, Pallas kernels, on_device(): pl.pallas_call(functools.partial(kernel, peers), out_shape=[pltpu.VMEM(di...  26 us
    pallas_call x1, Pallas kernels, on_device(): pl.pallas_call(write_out, out_shape=[jax.ShapeDtypeStruct(displacement.sh...  0.89 us

profile of v3, /device:TPU:0, one launch (start us, length us, event | category | flops | bytes accessed | tf_op | source)
XLA Modules:
  0.0 27.5 jit_solution(8999263185373000826)
XLA Ops:
  0.6 26.0 %shard_map.59 = (f32[4,3,32,256]{3,2,1,0:T(8,128)S(1)}, f32[4,3,32,256]{3,2,1,0:T(8,128)S(1)}) custom-call(f32[4,3,32,256]{3,2,1,0:T(8,128)} %disp.1, f32[4,3,32,256]{3,2,1,0:T(8,128)} %load.1, s32[4,32,256]{2,1,0:T(8,128)} %phase.1, f32[2,3]{1,0:T(2,128)} %moduli.1), custom_call_target="tpu_custom_call" | custom-call | tf_op jit(solution)/shard_map/pallas_call | solution.py:288
  26.6 0.9 %shard_map.60 = (f32[4,3,32,256]{3,2,1,0:T(8,128)}, f32[4,3,32,256]{3,2,1,0:T(8,128)}) custom-call(f32[4,3,32,256]{3,2,1,0:T(8,128)S(1)} %get-tuple-element.4.field, f32[4,3,32,256]{3,2,1,0:T(8,128)S(1)} %get-tuple-element.5.remain), custom_call_target="tpu_custom_call" | custom-call | tf_op jit(solution)/shard_map/pallas_call | solution.py:311
